TPU v7x, 32 devices: a whole 2x2x4 slice. The times are simulated.
32 devices in a mesh: expert: 2 (over y), tensor: 16 (over z, x, core).
Axes of the slice: x: 2, y: 2, z: 4, core: 2. Of those that a mesh axis runs over, the one named last changes fastest.
Arguments:
- tokens: bfloat16 [256, 6144], P(('expert', 'tensor')), may hold values from -6 to 6
- expert_ids: int32 [256, 2], P(('expert', 'tensor')), may hold values from 0 to 7, all different within a row; in each aligned block of 8 rows (0 to 7, 8 to 15, ...) at most 3 rows name the same one
- gates: float32 [256, 2], P(('expert', 'tensor')), may hold values from 0.2 to 1
- w_gate: bfloat16 [8, 6144, 8192], P('expert', None, 'tensor'), may hold values from -0.078125 to 0.078125
- w_up: bfloat16 [8, 6144, 8192], P('expert', None, 'tensor'), may hold values from -0.078125 to 0.078125
- w_down: bfloat16 [8, 8192, 6144], P('expert', 'tensor'), may hold values from -0.0625 to 0.0625
Outputs:
- mixed: bfloat16 [256, 6144], P(('expert', 'tensor'))
Inputs may be any that keep to these rules, and one draw needn't show every extreme that they name: `expert_ids`: each token names 2 different experts. Among the tokens of one device (aligned blocks of 8 rows) no expert is named more than 3 times, a bound that some expert reaches in every block.
All inputs are finite; a program needn't handle non-finite values.
Results may differ from a plain program's by a relative error of at most 0.02.
Values may be sent and summed in bfloat16 or wider, within the bound.
A program may use at most 128 MiB of HBM per device.

v0:
```python
import jax
import jax.numpy as jnp
from jax import lax
from jax.sharding import PartitionSpec as P

EXPERTS = 8
TOPK = 2
CAP = 3


def route_places(ids):
    flat = ids.reshape(-1)
    onehot = (flat[:, None] == jnp.arange(EXPERTS, dtype=jnp.int32)[None, :]).astype(jnp.int32)
    before = jnp.cumsum(onehot, axis=0) - onehot
    slot = jnp.sum(before * onehot, axis=1)
    return flat * CAP + slot


def body(tokens, expert_ids, gates, w_gate, w_up, w_down):
    n_groups = lax.axis_size("expert")
    local_experts = w_gate.shape[0]
    width = tokens.shape[1]
    tok_count = tokens.shape[0]
    places = route_places(expert_ids)
    picker = (jnp.arange(EXPERTS * CAP, dtype=jnp.int32)[:, None] == places[None, :]).astype(
        jnp.bfloat16
    )
    doubled = jnp.repeat(tokens, TOPK, axis=0)
    buffer = jnp.dot(picker, doubled, preferred_element_type=jnp.float32).astype(jnp.bfloat16)
    buffer = buffer.reshape(n_groups, local_experts * CAP, width)
    arrived = lax.all_to_all(buffer, "expert", split_axis=0, concat_axis=0, tiled=True)
    regrouped = arrived.reshape(n_groups, local_experts, CAP, width).transpose(1, 0, 2, 3)
    regrouped = regrouped.reshape(local_experts, n_groups * CAP, width)
    piece = lax.all_gather(regrouped, "tensor", axis=1, tiled=True)
    gate_act = jnp.einsum("erd,edf->erf", piece, w_gate, preferred_element_type=jnp.float32)
    up_act = jnp.einsum("erd,edf->erf", piece, w_up, preferred_element_type=jnp.float32)
    hidden = (jax.nn.silu(gate_act) * up_act).astype(jnp.bfloat16)
    piece = hidden
    term = jnp.einsum("erf,efd->red", piece, w_down, preferred_element_type=jnp.float32)
    summed = lax.psum_scatter(
        term.reshape(n_groups * CAP * lax.axis_size("tensor"), local_experts * width).astype(
            jnp.bfloat16
        ),
        "tensor",
        scatter_dimension=0,
        tiled=True,
    )
    results = summed.reshape(n_groups, CAP, local_experts, width)
    returned = lax.all_to_all(results, "expert", split_axis=0, concat_axis=0, tiled=True)
    results_flat = returned.transpose(0, 2, 1, 3).reshape(EXPERTS * CAP, width)
    weights = (jnp.arange(EXPERTS * CAP, dtype=jnp.int32)[None, :] == places[:, None]).astype(
        jnp.float32
    )
    weights = weights * gates.reshape(-1)[:, None]
    weights = jnp.sum(weights.reshape(tok_count, TOPK, EXPERTS * CAP), axis=1)
    mixed = jnp.dot(weights, results_flat.astype(jnp.float32), precision=lax.Precision.HIGHEST)
    return mixed.astype(jnp.bfloat16)


def solution(mesh):
    return jax.shard_map(
        body,
        mesh=mesh,
        in_specs=(
            P(("expert", "tensor"), None),
            P(("expert", "tensor"), None),
            P(("expert", "tensor"), None),
            P("expert", None, "tensor"),
            P("expert", None, "tensor"),
            P("expert", "tensor", None),
        ),
        out_specs=P(("expert", "tensor"), None),
        check_vma=False,
    )
```

profile of v0, /device:TPU:19, one launch (start us, length us, event | category | flops | bytes accessed | tf_op | source)
XLA Modules:
  0.0 246.6 jit_solution(2106851167836730849)
XLA Ops:
  6.5 0.0 all-gather.2.cloned.1.call-start
  6.5 0.8 copy.28
  7.3 0.1 eq.43
  7.4 0.1 fusion.12
  7.5 0.2 select_reduce_fusion.1
  7.7 1.0 broadcast_in_dim.2
  8.7 0.1 reshape.53
  8.8 0.2 convolution_convert_fusion.1
  9.0 0.1 reshape.54
  9.1 8.2 %all_to_all.10 = bf16[2,12,6144]{2,1,0:T(8,128)(2,1)S(1)} all-to-all(bf16[2,12,6144]{2,1,0:T(8,128)(2,1)S(1)} %reshape.54), channel_id=1, replica_groups=mesh['expert'=2,'tensor'=16] {'expert'}, dimensions={0} | all-to-all | bytes 589824 | tf_op jit(solution)/shard_map/all_to_all | solution.py:31
  17.3 0.3 copy.31
  17.6 0.9 copy.32
  18.5 0.0 all-gather.2.cloned.1.call-update
  18.5 53.3 %all-gather.2.cloned.1.call-done = bf16[4,96,6144]{2,0,1:T(4,128)(2,1)} async-done(((bf16[4,6,6144]{2,0,1:T(4,128)(2,1)}), bf16[4,96,6144]{2,0,1:T(4,128)(2,1)}) %all-gather.2.cloned.1.call-update) | async-done | bytes 4718608 | tf_op jit(solution)/shard_map/all_gather | solution.py:34
  71.8 0.0 copy-start
  71.8 14.0 %fusion.4 = f32[4,96,512]{2,1,0:T(8,128)S(1)} fusion(bf16[4,6144,512]{2,1,0:T(8,128)(2,1)} %param.9, bf16[4,96,6144]{2,0,1:T(4,128)(2,1)} %all-gather.2.cloned.1.call-done), kind=kOutput, calls=%fused_computation.6 | convolution fusion | flops 2415919104 | bytes 30670848 | tf_op jit(solution)/shard_map/erd,edf->erf/dot_general | solution.py:35
  85.9 0.0 copy-done
  85.9 15.0 %fusion.9 = bf16[4,96,512]{2,1,0:T(8,128)(2,1)S(1)} fusion(bf16[4,6144,512]{2,1,0:T(8,128)(2,1)} %param.10, bf16[4,96,6144]{2,0,1:T(4,128)(2,1)S(1)} %copy-done, f32[4,96,512]{2,1,0:T(8,128)S(1)} %fusion.4), kind=kOutput, calls=%fused_computation.9 | convolution fusion | flops 2417098752 | bytes 31064064 | tf_op jit(solution)/shard_map/erd,edf->erf/dot_general | solution.py:36
  100.8 12.5 %fusion.1 = bf16[4,12,8,6144]{3,2,1,0:T(8,128)(2,1)S(1)} fusion(bf16[4,96,512]{2,1,0:T(8,128)(2,1)S(1)} %fusion.9, bf16[4,512,6144]{2,1,0:T(8,128)(2,1)} %param.11), kind=kOutput, calls=%fused_computation.1 | convolution fusion | flops 2418278400 | bytes 30277632 | tf_op jit(solution)/shard_map/erf,efd->red/dot_general | solution.py:39
  113.3 0.0 copy-start.3
  113.3 2.6 %copy.37 = bf16[4,12,8,6144]{3,2,0,1:T(8,128)(2,1)} copy(bf16[4,12,8,6144]{3,2,1,0:T(8,128)(2,1)S(1)} %fusion.1) | data formatting | bytes 9437184 | tf_op jit(solution)/shard_map/convert_element_type | solution.py:41
  116.0 0.0 copy-start.2
  116.0 69.9 %fusion = bf16[8,24576]{1,0:T(8,128)(2,1)S(1)} fusion(bf16[96,24576]{1,0:T(8,128)(2,1)} %bitcast.19), kind=kCustom, calls=%all-reduce-scatter | all-reduce-scatter fusion | flops 3145729 | bytes 5112320
  185.8 6.1 %collective-permute-start.2 = (bf16[8,24576]{1,0:T(8,128)(2,1)S(1)}, bf16[8,24576]{1,0:T(8,128)(2,1)S(1)}, u32[]{:S(2)}, u32[]{:S(2)}) collective-permute-start(bf16[8,24576]{1,0:T(8,128)(2,1)S(1)} %fusion), channel_id=1, source_target_pairs={{0,3},{1,4},{2,5},{3,6},{4,7},{5,8},{6,9},{7,10},{8,11},{9,12},{10... | collective-permute-start | bytes 1179656
  192.0 1.9 collective-permute-start.1
  193.9 2.7 %collective-permute-start = (bf16[8,24576]{1,0:T(8,128)(2,1)S(1)}, bf16[8,24576]{1,0:T(8,128)(2,1)S(1)}, u32[]{:S(2)}, u32[]{:S(2)}) collective-permute-start(bf16[8,24576]{1,0:T(8,128)(2,1)S(1)} %fusion), channel_id=1, source_target_pairs={{0,1},{1,2},{2,3},{3,4},{4,5},{5,6},{6,7},{7,8},{8,9},{9,10},{10,1... | collective-permute-start | bytes 1179656
  196.6 0.1 slice
  196.7 1.9 collective-permute-start.3
  198.7 0.1 reduce_sum.21
  198.8 0.0 copy-done.3
  198.8 0.6 dynamic-slice.4
  200.0 22.6 %collective-permute-done.3 = bf16[6,24576]{1,0:T(8,128)(2,1)S(1)} collective-permute-done((bf16[6,24576]{1,0:T(8,128)(2,1)S(1)}, bf16[6,24576]{1,0:T(8,128)(2,1)S(1)}, u32[]{:S(2)}, u32[]{:S(2)}) %collective-permute-start.3) | collective-permute-done | bytes 294944
  222.6 0.0 copy-start.1
  222.6 0.0 collective-permute-done.2
  222.6 0.0 collective-permute-done.1
  222.6 0.7 copy-done.1
  223.3 0.0 collective-permute-done
  223.3 6.1 %concatenate = bf16[38,24576]{1,0:T(8,128)(2,1)S(1)} concatenate(bf16[6,24576]{1,0:T(8,128)(2,1)} %copy-done.1, bf16[8,24576]{1,0:T(8,128)(2,1)S(1)} %collective-permute-done.2, bf16[8,24576]{1,0:T(8,128)(2,1)S(1)} %collective-permute-done.1, bf16[8,24576]{1,0:T(8,128)(2,1)S(1)} %collective-permute-done, bf16[8,24576]{1,0:T(8,128)(2,1)S(1)} %fusion), dimensions={0} | concatenate | bytes 3735552
  229.4 0.1 constant_dynamic-slice_fusion
  229.6 1.1 reshape.57
  230.7 3.4 %all-to-all-start.1 = ((bf16[2,3,4,6144]{3,2,1,0:T(4,128)(2,1)}), bf16[2,3,4,6144]{3,2,1,0:T(4,128)(2,1)S(1)}, u32[]{:S(2)}, u32[]{:S(2)}) async-start(bf16[2,3,4,6144]{3,2,1,0:T(4,128)(2,1)} %reshape.57), calls=%async_computation.1 | async-start | bytes 589824 | tf_op jit(solution)/shard_map/all_to_all | solution.py:49
  234.2 0.1 copy.30
  234.2 0.0 copy-done.2
  234.2 0.1 select_reduce_fusion
  234.3 4.0 %all-to-all-done.1 = bf16[2,3,4,6144]{3,2,1,0:T(4,128)(2,1)S(1)} async-done(((bf16[2,3,4,6144]{3,2,1,0:T(4,128)(2,1)}), bf16[2,3,4,6144]{3,2,1,0:T(4,128)(2,1)S(1)}, u32[]{:S(2)}, u32[]{:S(2)}) %all-to-all-start.1) | async-done | bytes 294944 | tf_op jit(solution)/shard_map/all_to_all | solution.py:49
  238.3 0.3 copy.36
  238.6 0.3 reshape.58
  238.8 0.9 convolution_convert_fusion.2
  (3 shorter events, 0.0 us)
Async XLA Ops:
  6.5 65.3 %all-gather.2.cloned.1.call-start = ((), (), s32[]{:S(2)}) async-start(), calls=%async_computation.2 | async-start | bytes 5013504 | tf_op jit(solution)/shard_map/all_gather | solution.py:34
  71.8 14.0 %copy-start = (bf16[4,96,6144]{2,0,1:T(4,128)(2,1)S(1)}, bf16[4,96,6144]{2,0,1:T(4,128)(2,1)}, u32[]{:S(2)}) copy-start(bf16[4,96,6144]{2,0,1:T(4,128)(2,1)} %all-gather.2.cloned.1.call-done) | copy-start | bytes 14155780
  113.3 85.4 %copy-start.3 = (u32[32]{0:T(128)S(1)}, u32[32]{0:T(128)}, u32[]{:S(2)}) copy-start(u32[32]{0:T(128)} %constant.19) | copy-start | bytes 388
  116.0 118.3 %copy-start.2 = (f32[8,2]{0,1:T(2,128)S(1)}, f32[8,2]{0,1:T(2,128)}, u32[]{:S(2)}) copy-start(f32[8,2]{0,1:T(2,128)} %param.8) | copy-start | bytes 196
  185.8 36.7 %collective-permute-start.2 = (bf16[8,24576]{1,0:T(8,128)(2,1)S(1)}, bf16[8,24576]{1,0:T(8,128)(2,1)S(1)}, u32[]{:S(2)}, u32[]{:S(2)}) collective-permute-start(bf16[8,24576]{1,0:T(8,128)(2,1)S(1)} %fusion), channel_id=1, source_target_pairs={{0,3},{1,4},{2,5},{3,6},{4,7},{5,8},{6,9},{7,10},{8,11},{9,12},{10... | collective-permute-start | bytes 1179656
  192.0 30.6 %collective-permute-start.1 = (bf16[8,24576]{1,0:T(8,128)(2,1)S(1)}, bf16[8,24576]{1,0:T(8,128)(2,1)S(1)}, u32[]{:S(2)}, u32[]{:S(2)}) collective-permute-start(bf16[8,24576]{1,0:T(8,128)(2,1)S(1)} %fusion), channel_id=1, source_target_pairs={{0,2},{1,3},{2,4},{3,5},{4,6},{5,7},{6,8},{7,9},{8,10},{9,11},{10,... | collective-permute-start | bytes 1179656
  193.9 29.4 %collective-permute-start = (bf16[8,24576]{1,0:T(8,128)(2,1)S(1)}, bf16[8,24576]{1,0:T(8,128)(2,1)S(1)}, u32[]{:S(2)}, u32[]{:S(2)}) collective-permute-start(bf16[8,24576]{1,0:T(8,128)(2,1)S(1)} %fusion), channel_id=1, source_target_pairs={{0,1},{1,2},{2,3},{3,4},{4,5},{5,6},{6,7},{7,8},{8,9},{9,10},{10,1... | collective-permute-start | bytes 1179656
  196.7 25.8 %collective-permute-start.3 = (bf16[6,24576]{1,0:T(8,128)(2,1)S(1)}, bf16[6,24576]{1,0:T(8,128)(2,1)S(1)}, u32[]{:S(2)}, u32[]{:S(2)}) collective-permute-start(bf16[6,24576]{1,0:T(8,128)(2,1)S(1)} %slice), channel_id=1, source_target_pairs={{0,4},{1,5},{2,6},{3,7},{4,8},{5,9},{6,10},{7,11},{8,12},{9,13},{1... | collective-permute-start | bytes 884744
  222.6 0.7 copy-start.1
  230.7 7.6 %all-to-all-start.1 = ((bf16[2,3,4,6144]{3,2,1,0:T(4,128)(2,1)}), bf16[2,3,4,6144]{3,2,1,0:T(4,128)(2,1)S(1)}, u32[]{:S(2)}, u32[]{:S(2)}) async-start(bf16[2,3,4,6144]{3,2,1,0:T(4,128)(2,1)} %reshape.57), calls=%async_computation.1 | async-start | bytes 589824 | tf_op jit(solution)/shard_map/all_to_all | solution.py:49
Sparse Core Ops, SparseCore 0:
  18.6 53.1 all-gather.1
where the time goes:
time: 247 us
  waiting for transfers between devices  79.9 us (32%)
  blocking collectives  78.1 us (32%)
  matrix products  42.6 us (17%)
  starting transfers between devices  16.1 us (7%)
  local copies, waits for them, and re-layouts  15.3 us (6%)
  between operations  14.2 us (6%)
    unnamed x1, blocking collectives  69.9 us
    all_gather x1, waiting for transfers between devices, body(): piece = lax.all_gather(regrouped, 'tensor', axis=1, tiled=True)  53.3 us
    unnamed x5, waiting for transfers between devices  22.6 us
    dot_general x1, matrix products, body(): jnp.einsum('erd,edf->erf', piece, w_up, preferred_element_type=jnp.float32)  15 us
    dot_general x1, matrix products, body(): jnp.einsum('erd,edf->erf', piece, w_gate, preferred_element_type=jnp.floa...  14 us
    unnamed x4, starting transfers between devices  12.7 us
    dot_general x1, matrix products, body(): jnp.einsum('erf,efd->red', piece, w_down, preferred_element_type=jnp.floa...  12.5 us
    unnamed x13, local copies, waits for them, and re-layouts  8.41 us
  transfers between devices with their start and end apart: 6, of which 3 were waited for; matrix products, arithmetic and copies ran while one was open for 0% of the time, Pallas kernels for 0%

commit v1 on v0

--- a/solution.py
+++ b/solution.py
@@ -1,11 +1,19 @@
+import functools
+
 import jax
 import jax.numpy as jnp
 from jax import lax
+from jax.experimental import pallas as pl
+from jax.experimental.pallas import tpu as pltpu
 from jax.sharding import PartitionSpec as P
 
 EXPERTS = 8
 TOPK = 2
 CAP = 3
+LANES = 128
+SUB = 512
+SLOTS = 6
+ORDER = (1, 3, 2)
 
 
 def route_places(ids):
@@ -16,7 +24,7 @@
     return flat * CAP + slot
 
 
-def body(tokens, expert_ids, gates, w_gate, w_up, w_down):
+def plain_body(tokens, expert_ids, gates, w_gate, w_up, w_down):
     n_groups = lax.axis_size("expert")
     local_experts = w_gate.shape[0]
     width = tokens.shape[1]
@@ -35,8 +43,7 @@
     gate_act = jnp.einsum("erd,edf->erf", piece, w_gate, preferred_element_type=jnp.float32)
     up_act = jnp.einsum("erd,edf->erf", piece, w_up, preferred_element_type=jnp.float32)
     hidden = (jax.nn.silu(gate_act) * up_act).astype(jnp.bfloat16)
-    piece = hidden
-    term = jnp.einsum("erf,efd->red", piece, w_down, preferred_element_type=jnp.float32)
+    term = jnp.einsum("erf,efd->red", hidden, w_down, preferred_element_type=jnp.float32)
     summed = lax.psum_scatter(
         term.reshape(n_groups * CAP * lax.axis_size("tensor"), local_experts * width).astype(
             jnp.bfloat16
@@ -55,6 +62,327 @@
     weights = jnp.sum(weights.reshape(tok_count, TOPK, EXPERTS * CAP), axis=1)
     mixed = jnp.dot(weights, results_flat.astype(jnp.float32), precision=lax.Precision.HIGHEST)
     return mixed.astype(jnp.bfloat16)
+
+
+def kernel(
+    dims,
+    tok, wg, wu, wd, out,
+    raw, xs, route, gbuf, ubuf, dbuf, gacc, uacc, hid,
+    own, p1, s1, t3, ra, rb, t1, t2, rx, ry, t0, rz,
+    gsem, usem, dsem,
+    zs, zr, xsend, xrecv, ysend, yrecv, das, dar, dbs, dbr, ss, sr,
+    r1s, r1r, r2s, r2r, r3s, r3r, r4s, r4r,
+):
+    n_exp, width, kc, n_k, nz, rows8 = dims
+    f32, bf16 = jnp.float32, jnp.bfloat16
+    wide = tok.shape[1]
+    cut = (width // 2 // LANES) * LANES
+    n_steps = n_exp * n_k
+    n_sub = width // SUB
+    n_chunk = n_sub // 2
+    quarter = nz * rows8
+    half = 4 * quarter
+
+    y = lax.axis_index("expert")
+    t = lax.axis_index("tensor")
+    z, x, c = t // 4, (t // 2) % 2, t % 2
+
+    def at(yy, zz, xx, cc):
+        return (yy, (zz * 2 + xx) * 2 + cc)
+
+    xn = at(y, z, 1 - x, c)
+    yn = at(1 - y, z, x, c)
+    sib = at(y, z, x, 1 - c)
+    zn = [at(y, (z + k) % nz, x, c) for k in range(nz)]
+
+    def load_g(s, slot):
+        rows = pl.ds(pl.multiple_of((s % n_k) * kc, kc), kc)
+        e = s // n_k
+        return (
+            pltpu.make_async_copy(wg.at[e, rows, :], gbuf.at[slot], gsem.at[slot]),
+            pltpu.make_async_copy(wu.at[e, rows, :], ubuf.at[slot], usem.at[slot]),
+        )
+
+    def load_d(n):
+        cols = pl.ds(pl.multiple_of(n * SUB, SUB), SUB)
+        return pltpu.make_async_copy(wd.at[:, :, cols], dbuf.at[n], dsem.at[n])
+
+    for s in range(SLOTS):
+        for copy in load_g(s, s):
+            copy.start()
+    for n in range(n_sub):
+        load_d(n).start()
+
+    barrier = pltpu.get_barrier_semaphore()
+    peers = [xn, yn, sib] + zn[1:]
+    for peer in peers:
+        pl.semaphore_signal(barrier, inc=1, device_id=peer, device_id_type=pl.DeviceIdType.MESH)
+    pl.semaphore_wait(barrier, len(peers))
+
+    sent = []
+
+    def send(src, dst, ssem, rsem, dev):
+        copy = pltpu.make_async_remote_copy(
+            src_ref=src, dst_ref=dst, send_sem=ssem, recv_sem=rsem,
+            device_id=dev, device_id_type=pl.DeviceIdType.MESH,
+        )
+        copy.start()
+        sent.append(copy)
+        return copy
+
+    def mine(j):
+        return tok if j == 0 else raw.at[0, 0, j]
+
+    def to_sib(g, j):
+        src = mine(j) if g == 0 else raw.at[0, g, j]
+        return send(src, raw.at[1, g, j], ss.at[g, j], sr.at[g, j], sib)
+
+    zc, xc, yc, sc, ac, bc = {}, {}, {}, {}, {}, {}
+    for k in ORDER:
+        j = (nz - k) % nz
+        zc[j] = send(tok, raw.at[0, 0, j], zs.at[k], zr.at[j], zn[k])
+
+    def spread(j):
+        xc[j] = send(mine(j), raw.at[0, 1, j], xsend.at[j], xrecv.at[j], xn)
+        yc[j] = send(mine(j), raw.at[0, 2, j], ysend.at[j], yrecv.at[j], yn)
+        sc[0, j] = to_sib(0, j)
+
+    spread(0)
+    raw[0, 0, 0] = tok[...]
+    for j in ORDER:
+        zc[j].wait_recv()
+        spread(j)
+    for j in (0,) + ORDER:
+        xc[j].wait_recv()
+        ac[j] = send(
+            raw.at[0, 1, j, :, pl.ds(0, cut)], raw.at[0, 3, j, :, pl.ds(0, cut)],
+            das.at[j], dar.at[j], yn,
+        )
+        sc[1, j] = to_sib(1, j)
+        yc[j].wait_recv()
+        bc[j] = send(
+            raw.at[0, 2, j, :, pl.ds(cut, wide - cut)], raw.at[0, 3, j, :, pl.ds(cut, wide - cut)],
+            dbs.at[j], dbr.at[j], xn,
+        )
+        sc[2, j] = to_sib(2, j)
+
+    def settle(a, g):
+        r0 = (a * 4 + g) * quarter
+
+        def part(i, _):
+            cols = pl.ds(pl.multiple_of(i * SUB, SUB), SUB)
+            v = raw[a, g, :, :, cols].astype(f32).reshape(quarter, SUB)
+            xs[r0:r0 + quarter, cols] = v.astype(bf16)
+            return 0
+
+        lax.fori_loop(0, width // SUB, part, 0)
+        v = raw[a, g, :, :, width:wide].astype(f32)
+        route[r0:r0 + quarter, :] = v.reshape(quarter, wide - width)
+
+    for g in range(3):
+        settle(0, g)
+    for g in range(3):
+        for j in range(nz):
+            sc[g, j].wait_recv()
+        settle(1, g)
+    for j in (0,) + ORDER:
+        ac[j].wait_recv()
+        bc[j].wait_recv()
+        sc[3, j] = to_sib(3, j)
+    settle(0, 3)
+    for j in range(nz):
+        sc[3, j].wait_recv()
+    settle(1, 3)
+
+    def step(s, _):
+        slot = s % SLOTS
+        for copy in load_g(s, slot):
+            copy.wait()
+        k = s % n_k
+        e = s // n_k
+        left = xs[:, pl.ds(pl.multiple_of(k * kc, kc), kc)]
+        g = jnp.dot(left, gbuf[slot], preferred_element_type=f32)
+        u = jnp.dot(left, ubuf[slot], preferred_element_type=f32)
+
+        @pl.when(k == 0)
+        def _():
+            gacc[...] = g
+            uacc[...] = u
+
+        @pl.when(k > 0)
+        def _():
+            gacc[...] += g
+            uacc[...] += u
+
+        @pl.when(s + SLOTS < n_steps)
+        def _():
+            for copy in load_g(s + SLOTS, slot):
+                copy.start()
+
+        @pl.when(k == n_k - 1)
+        def _():
+            lane = lax.broadcasted_iota(jnp.int32, route.shape, 1)
+            which = y * n_exp + e
+            hit = (lane == which) | (lane == which + EXPERTS)
+            w = jnp.sum(jnp.where(hit, route[...], 0.0), axis=1, keepdims=True)
+            gv = gacc[...]
+            hid[e] = (gv / (1.0 + jnp.exp(-gv)) * uacc[...] * w).astype(bf16)
+
+        return 0
+
+    lax.fori_loop(0, n_steps, step, 0)
+
+    def down(n, _):
+        load_d(n).wait()
+        acc = jnp.dot(hid[0], dbuf[n, 0], preferred_element_type=f32)
+        for e in range(1, n_exp):
+            acc += jnp.dot(hid[e], dbuf[n, e], preferred_element_type=f32)
+        own[n] = acc[:half]
+        p1[n] = acc[half:].astype(bf16)
+        return 0
+
+    c1, c2, c3, c4 = {}, {}, {}, {}
+    q = quarter
+
+    def stage1(i):
+        lax.fori_loop(2 * i, 2 * i + 2, down, 0)
+        two = pl.ds(2 * i, 2)
+        c1[i] = send(p1.at[two], s1.at[two], r1s.at[i], r1r.at[i], sib)
+
+    def stage2(i):
+        a, b = 2 * i, 2 * i + 1
+        c1[i].wait_recv()
+        for n in (a, b):
+            t3[n] = (own[n, 3 * q:4 * q] + s1[n, 3 * q:4 * q].astype(f32)).astype(bf16)
+        c2[i] = (
+            send(t3.at[a], ra.at[i], r2s.at[i, 0], r2r.at[i, 0], yn),
+            send(t3.at[b], rb.at[i], r2s.at[i, 1], r2r.at[i, 1], xn),
+        )
+        for n in (a, b):
+            own[n, 0:3 * q] += s1[n, 0:3 * q].astype(f32)
+
+    def stage3(i):
+        a, b = 2 * i, 2 * i + 1
+        for copy in c2[i]:
+            copy.wait_recv()
+        t1[a] = (own[a, q:2 * q] + ra[i].astype(f32)).astype(bf16)
+        t1[b] = own[b, q:2 * q].astype(bf16)
+        t2[a] = own[a, 2 * q:3 * q].astype(bf16)
+        t2[b] = (own[b, 2 * q:3 * q] + rb[i].astype(f32)).astype(bf16)
+        two = pl.ds(a, 2)
+        c3[i] = (
+            send(t1.at[two], rx.at[two], r3s.at[i, 0], r3r.at[i, 0], xn),
+            send(t2.at[two], ry.at[two], r3s.at[i, 1], r3r.at[i, 1], yn),
+        )
+
+    def stage4(i):
+        for copy in c3[i]:
+            copy.wait_recv()
+        for n in (2 * i, 2 * i + 1):
+            v = own[n, 0:q] + rx[n].astype(f32) + ry[n].astype(f32)
+            own[n, 0:q] = v
+            v = v.reshape(nz, rows8, SUB).astype(bf16)
+            for k in range(1, nz):
+                t0[k, n] = v[k]
+        two = pl.ds(2 * i, 2)
+        c4[i] = [
+            send(t0.at[k, two], rz.at[k, two], r4s.at[i, k], r4r.at[i, k], zn[k])
+            for k in range(1, nz)
+        ]
+
+    def stage5(i):
+        for copy in c4[i]:
+            copy.wait_recv()
+        for n in (2 * i, 2 * i + 1):
+            v = own[n, 0:rows8]
+            for k in range(1, nz):
+                v += rz[k, n].astype(f32)
+            out[:, n * SUB:(n + 1) * SUB] = v.astype(out.dtype)
+
+    stages = (stage1, stage2, stage3, stage4, stage5)
+    for tick in range(n_chunk + len(stages) - 1):
+        for lag, stage in enumerate(stages):
+            if 0 <= tick - lag < n_chunk:
+                stage(tick - lag)
+    for copy in sent:
+        copy.wait_send()
+
+
+def fused_body(tokens, expert_ids, gates, w_gate, w_up, w_down):
+    rows8, width = tokens.shape
+    n_exp, _, ff = w_gate.shape
+    n_tensor = lax.axis_size("tensor")
+    nz = n_tensor // 4
+    n_k = 4
+    kc = width // n_k
+    bf16, f32 = jnp.bfloat16, jnp.float32
+    lanes = jnp.arange(EXPERTS, dtype=jnp.int32)
+    full = jnp.sum(
+        jnp.where(expert_ids[:, :, None] == lanes[None, None, :], gates[:, :, None], 0.0), axis=1
+    )
+    top = full.astype(bf16)
+    low = (full - top.astype(f32)).astype(bf16)
+    pad = jnp.zeros((rows8, LANES - 2 * EXPERTS), bf16)
+    tok = jnp.concatenate([tokens, top, low, pad], axis=1)
+    wide = width + LANES
+    rows = 8 * nz * rows8
+    q = nz * rows8
+    n_sub = width // SUB
+    n_chunk = n_sub // 2
+    dma = pltpu.SemaphoreType.DMA
+    vm = pltpu.VMEM
+    scratch = [
+        vm((2, 4, nz, rows8, wide), bf16),
+        vm((rows, width), bf16),
+        vm((rows, LANES), f32),
+        vm((SLOTS, kc, ff), bf16),
+        vm((SLOTS, kc, ff), bf16),
+        vm((n_sub, n_exp, ff, SUB), bf16),
+        vm((rows, ff), f32),
+        vm((rows, ff), f32),
+        vm((n_exp, rows, ff), bf16),
+        vm((n_sub, 4 * q, SUB), f32),
+        vm((n_sub, 4 * q, SUB), bf16),
+        vm((n_sub, 4 * q, SUB), bf16),
+        vm((n_sub, q, SUB), bf16),
+        vm((n_chunk, q, SUB), bf16),
+        vm((n_chunk, q, SUB), bf16),
+        vm((n_sub, q, SUB), bf16),
+        vm((n_sub, q, SUB), bf16),
+        vm((n_sub, q, SUB), bf16),
+        vm((n_sub, q, SUB), bf16),
+        vm((nz, n_sub, rows8, SUB), bf16),
+        vm((nz, n_sub, rows8, SUB), bf16),
+        dma((SLOTS,)), dma((SLOTS,)), dma((n_sub,)),
+        dma((nz,)), dma((nz,)), dma((nz,)), dma((nz,)), dma((nz,)), dma((nz,)),
+        dma((nz,)), dma((nz,)), dma((nz,)), dma((nz,)), dma((4, nz)), dma((4, nz)),
+        dma((n_chunk,)), dma((n_chunk,)), dma((n_chunk, 2)), dma((n_chunk, 2)),
+        dma((n_chunk, 2)), dma((n_chunk, 2)), dma((n_chunk, nz)), dma((n_chunk, nz)),
+    ]
+    return pl.pallas_call(
+        functools.partial(kernel, (n_exp, width, kc, n_k, nz, rows8)),
+        out_shape=jax.ShapeDtypeStruct((rows8, width), bf16),
+        in_specs=[pl.BlockSpec(memory_space=pltpu.VMEM)]
+        + [pl.BlockSpec(memory_space=pl.ANY)] * 3,
+        out_specs=pl.BlockSpec(memory_space=pltpu.VMEM),
+        scratch_shapes=scratch,
+        compiler_params=pltpu.CompilerParams(
+            collective_id=0, has_side_effects=True, vmem_limit_bytes=67043328
+        ),
+    )(tok, w_gate, w_up, w_down)
+
+
+def body(tokens, expert_ids, gates, w_gate, w_up, w_down):
+    fits = (
+        lax.axis_size("expert") == 2
+        and lax.axis_size("tensor") == 16
+        and tokens.shape[0] == 8
+        and w_gate.size * 2 <= 32 * 1024 * 1024
+        and w_gate.shape[2] == SUB
+        and tokens.shape[1] % (2 * SUB) == 0
+    )
+    run = fused_body if fits else plain_body
+    return run(tokens, expert_ids, gates, w_gate, w_up, w_down)
 
 
 def solution(mesh):

time: 247 us -> 78 us (0.32)
  the two profiles are of different devices: /device:TPU:19 before, /device:TPU:0 now
where the time goes in v1:
time: 78 us; the launch traced here: 77.8 us
  Pallas kernels  73.8 us (95%)
  local copies, waits for them, and re-layouts  3.16 us (4%)
  other arithmetic  0.78 us (1%)
    pallas_call x1, Pallas kernels, fused_body(): pl.pallas_call(functools.partial(kernel, (n_exp, width, kc, n_k, nz, rows...  73.8 us
    concatenate x1, local copies, waits for them, and re-layouts, fused_body(): tok = jnp.concatenate([tokens, top, low, pad], axis=1)  1.61 us

profile of v1, /device:TPU:0, one launch (start us, length us, event | category | flops | bytes accessed | tf_op | source)
XLA Modules:
  0.0 77.8 jit_solution(8738880162752119411)
XLA Ops:
  0.0 0.8 select_reduce_fusion
  0.8 1.6 %concatenate.3.tok = bf16[8,6272]{1,0:T(8,128)(2,1)} concatenate(bf16[8,6144]{1,0:T(8,128)(2,1)} %param.6, bf16[8,8]{1,0:T(8,128)(2,1)S(1)} %get-tuple-element.6, bf16[8,8]{1,0:T(8,128)(2,1)S(1)} %get-tuple-element.5, bf16[8,112]{1,0:T(8,128)(2,1)S(1)} %broadcast_in_dim.20), dimensions={1} | concatenate | bytes 200704 | tf_op jit(solution)/shard_map/concatenate | solution.py:326
  2.4 73.8 %shard_map.64 = bf16[8,6144]{1,0:T(8,128)(2,1)} custom-call(bf16[8,6272]{1,0:T(8,128)(2,1)} %concatenate.3.tok, bf16[4,6144,512]{2,1,0:T(8,128)(2,1)} %wg.1, bf16[4,6144,512]{2,1,0:T(8,128)(2,1)} %wu.1, bf16[4,512,6144]{2,1,0:T(8,128)(2,1)} %wd.1), custom_call_target="tpu_custom_call" | custom-call | tf_op jit(solution)/shard_map/pallas_call | solution.py:362
  76.2 1.5 %copy.10 = bf16[8,6144]{1,0:T(8,128)(2,1)} copy(bf16[8,6144]{1,0:T(8,128)(2,1)} %shard_map.64) | data formatting | bytes 196608
  (2 shorter events, 0.0 us)
